TPU v7x, 32 devices: a whole 2x2x4 slice. The times are simulated.
32 devices in a mesh: row: 8 (over z, x), col: 2 (over y), depth: 2 (over core).
Axes of the slice: x: 2, y: 2, z: 4, core: 2. Of those that a mesh axis runs over, the one named last changes fastest.
Arguments:
- tokens: bfloat16 [1024, 5376], P('row', 'depth'), may hold values from -6 to 6
- gate_weight: bfloat16 [9216, 5376], P(('col', 'row'), 'depth'), may hold values from -0.078125 to 0.078125
- up_weight: bfloat16 [9216, 5376], P(('col', 'row'), 'depth'), may hold values from -0.078125 to 0.078125
- down_weight: bfloat16 [9216, 5376], P(('col', 'depth'), 'row'), may hold values from -0.09375 to 0.09375
Outputs:
- output: bfloat16 [1024, 5376], P('row', ('col', 'depth'))
All inputs are finite; a program needn't handle non-finite values.
Results may differ from a plain program's by a relative error of at most 0.0049.
Values may be sent and summed in bfloat16 or wider, within the bound.
A program may use at most 128 MiB of HBM per device.

v0:
```python
import jax
import jax.numpy as jnp
from jax import lax
from jax.sharding import PartitionSpec as P


def local(tokens, gate_weight, up_weight, down_weight):
    paired = jnp.stack([gate_weight, up_weight])
    every_token = jnp.einsum(
        "td,gfd->gtf",
        lax.all_gather(tokens, "row", axis=0, tiled=True),
        paired,
        preferred_element_type=jnp.float32,
    )
    partial_sums = lax.all_to_all(every_token, "row", split_axis=1, concat_axis=2, tiled=True)
    share_width = partial_sums.shape[2] // lax.axis_size("depth")
    summed = lax.psum(partial_sums, "depth")
    shares = lax.dynamic_slice_in_dim(summed, lax.axis_index("depth") * share_width, share_width, 2)
    hidden = (jax.nn.silu(shares[0]) * shares[1]).astype(jnp.bfloat16)
    down_terms = jnp.dot(
        hidden,
        lax.all_gather(down_weight, "row", axis=1, tiled=True),
        preferred_element_type=jnp.float32,
    )
    return lax.psum_scatter(down_terms, ("col", "depth"), scatter_dimension=1, tiled=True).astype(
        jnp.bfloat16
    )


def solution(mesh):
    in_specs = (
        P("row", "depth"),
        P(("col", "row"), "depth"),
        P(("col", "row"), "depth"),
        P(("col", "depth"), "row"),
    )
    out_specs = P("row", ("col", "depth"))
    return jax.shard_map(local, mesh=mesh, in_specs=in_specs, out_specs=out_specs, check_vma=False)
```

profile of v0, /device:TPU:0, one launch (start us, length us, event | category | flops | bytes accessed | tf_op | source)
XLA Modules:
  0.0 810.8 jit_solution(2922904456121408201)
XLA Ops:
  6.5 0.0 all-gather.3.cloned.1.call-start
  6.5 0.7 all-gather.3.cloned.1.call-update
  7.3 0.0 all-reduce.2.cloned.1.call-start
  7.3 94.1 %all-gather.3.cloned.1.call-done = bf16[1024,2688]{1,0:T(8,128)(2,1)} async-done(((bf16[128,2688]{1,0:T(8,128)(2,1)}), bf16[1024,2688]{1,0:T(8,128)(2,1)}) %all-gather.3.cloned.1.call-update) | async-done | bytes 5505040 | tf_op jit(solution)/shard_map/all_gather | solution.py:11
  101.4 12.0 %fusion.5 = f32[2,1024,576]{1,2,0:T(8,128)} fusion(bf16[1024,2688]{1,0:T(8,128)(2,1)} %all-gather.3.cloned.1.call-done, bf16[1,576,2688]{2,1,0:T(8,128)(2,1)} %bitcast.29, bf16[1,576,2688]{2,1,0:T(8,128)(2,1)} %bitcast.30), kind=kOutput, calls=%fused_computation.5 | convolution fusion | flops 6344884224 | bytes 16416768 | tf_op jit(solution)/shard_map/td,gfd->gtf/dot_general | solution.py:9
  113.4 8.8 %copy.7 = f32[2,1024,576]{2,0,1:T(2,128)} copy(f32[2,1024,576]{1,2,0:T(8,128)} %fusion.5) | data formatting | bytes 9437184 | tf_op jit(solution)/shard_map/td,gfd->gtf/transpose | solution.py:9
  122.1 118.9 %all_to_all.18 = f32[2,1024,576]{2,0,1:T(2,128)} all-to-all(f32[2,1024,576]{2,0,1:T(2,128)} %copy.7), channel_id=1, replica_groups=mesh['row'=8,'col'=2,'depth'=2] {'row'}, dimensions={1} | all-to-all | bytes 9437184 | tf_op jit(solution)/shard_map/all_to_all | solution.py:15
  241.1 8.7 %copy.11 = f32[2,8,128,576]{2,3,1,0:T(8,128)} copy(f32[2,8,128,576]{3,0,2,1:T(2,128)} %bitcast.27) | data formatting | bytes 9437184 | tf_op jit(solution)/shard_map/all_to_all | solution.py:15
  249.7 0.0 all-reduce.2.cloned.1.call-update
  249.8 0.0 all-gather.5.cloned.1.call-start
  249.8 0.7 all-gather.5.cloned.1.call-update
  250.5 0.0 reduce-scatter.2.cloned.1.call-start
  250.6 27.2 %all-reduce.2.cloned.1.call-done = f32[2,128,4608]{1,2,0:T(8,128)} async-done(((f32[2,128,4608]{1,2,0:T(8,128)}), f32[2,128,4608]{1,2,0:T(8,128)}) %all-reduce.2.cloned.1.call-update) | async-done | bytes 4718608 | tf_op jit(solution)/shard_map/psum | solution.py:17
  277.8 475.7 %all-gather.5.cloned.1.call-done = bf16[2304,5376]{0,1:T(8,128)(2,1)} async-done(((bf16[2304,672]{0,1:T(8,128)(2,1)}), bf16[2304,5376]{0,1:T(8,128)(2,1)}) %all-gather.5.cloned.1.call-update) | async-done | bytes 24772624 | tf_op jit(solution)/shard_map/all_gather | solution.py:22
  753.5 13.3 %fusion.12 = f32[128,5376]{0,1:T(8,128)} fusion(bf16[2304,5376]{0,1:T(8,128)(2,1)} %all-gather.5.cloned.1.call-done, f32[2,128,4608]{1,2,0:T(8,128)} %all-reduce.2.cloned.1.call-done, s32[]{:T(128)S(6)} %add.13, s32[]{:T(128)S(6)} %select_n.3), kind=kOutput, calls=%fused_computation.10 | convolution fusion | flops 3172663296 | bytes 29884424 | tf_op jit(solution)/shard_map/dot_general | solution.py:20
  766.9 0.0 reduce-scatter.2.cloned.1.call-update
  766.9 35.5 %reduce-scatter.2.cloned.1.call-done = f32[128,1344]{0,1:T(8,128)} async-done(((f32[128,5376]{0,1:T(8,128)}), f32[128,1344]{0,1:T(8,128)}) %reduce-scatter.2.cloned.1.call-update) | async-done | bytes 688144 | tf_op jit(solution)/shard_map/reduce_scatter | solution.py:25
  802.4 1.9 convert_element_type.7
Async XLA Ops:
  6.5 94.9 %all-gather.3.cloned.1.call-start = ((), (), s32[]{:S(2)}) async-start(), calls=%async_computation.2 | async-start | bytes 6193152 | tf_op jit(solution)/shard_map/all_gather | solution.py:11
  7.3 270.5 %all-reduce.2.cloned.1.call-start = ((), (), s32[]{:S(2)}) async-start(), calls=%async_computation.3 | async-start | bytes 9437184 | tf_op jit(solution)/shard_map/psum | solution.py:17
  249.8 503.8 %all-gather.5.cloned.1.call-start = ((), (), s32[]{:S(2)}) async-start(), calls=%async_computation.4 | async-start | bytes 27869184 | tf_op jit(solution)/shard_map/all_gather | solution.py:22
  250.5 551.9 %reduce-scatter.2.cloned.1.call-start = ((), (), s32[]{:S(2)}) async-start(), calls=%async_computation.5 | async-start | bytes 3440640 | tf_op jit(solution)/shard_map/reduce_scatter | solution.py:25
Sparse Core Ops, SparseCore 0:
  9.5 91.8 all-gather.2
  249.9 27.8 all-reduce.1
  279.3 474.1 all-gather.4
  767.0 35.2 reduce-scatter.1
where the time goes:
time: 811 us
  waiting for transfers between devices  634 us (78%)
  blocking collectives  119 us (15%)
  matrix products  25.3 us (3%)
  local copies, waits for them, and re-layouts  17.5 us (2%)
  between operations  13.1 us (2%)
    all_gather x1, waiting for transfers between devices, local(): lax.all_gather(down_weight, 'row', axis=1, tiled=True)  476 us
    all_to_all x1, blocking collectives, local(): lax.all_to_all(every_token, 'row', split_axis=1, concat_axis=2, tiled=True)  119 us
    all_gather x1, waiting for transfers between devices, local(): lax.all_gather(tokens, 'row', axis=0, tiled=True)  94.1 us
    reduce_scatter x1, waiting for transfers between devices, local(): lax.psum_scatter(down_terms, ('col', 'depth'), scatter_dimension=1, tiled...  35.5 us
    psum x1, waiting for transfers between devices, local(): summed = lax.psum(partial_sums, 'depth')  27.2 us
  transfers between devices with their start and end apart: 4, of which 4 were waited for; matrix products, arithmetic and copies ran while one was open for 0% of the time, Pallas kernels for 0%

commit v1 on v0

--- a/solution.py
+++ b/solution.py
@@ -2,6 +2,32 @@
 import jax.numpy as jnp
 from jax import lax
 from jax.sharding import PartitionSpec as P
+
+
+def _change_edges(shard_in, axis_k, array_here):
+    tmp, carry_in = (shard_in.shape[:axis_k], shard_in.shape[axis_k + 1 :])
+    near = shard_in.reshape(*tmp, array_here, -1, *carry_in)
+    return jnp.moveaxis(near, axis_k, 0)
+
+
+def _run_screen(xs, dim_no):
+    xs = jnp.moveaxis(xs, 0, dim_no)
+    val2 = xs.shape
+    return xs.reshape(*val2[:dim_no], val2[dim_no] * val2[dim_no + 1], *val2[dim_no + 2 :])
+
+
+def _begin_slots(piece_in, axis_id, vector, target):
+    r1 = lax.axis_size(axis_id)
+    block_out = lax.axis_index(axis_id)
+    after, x_now = (r1, block_out)
+    piece_now = _change_edges(piece_in, vector, after)
+    side_arr = piece_now
+    for rr in range(1, after):
+        v_next, f_now = ((x_now + rr) % after, (x_now - rr) % after)
+        spare = lax.dynamic_index_in_dim(piece_now, v_next, 0)
+        taken_in = lax.ppermute(spare, axis_id, [(pp, (pp + rr) % after) for pp in range(after)])
+        side_arr = lax.dynamic_update_slice_in_dim(side_arr, taken_in, f_now, axis=0)
+    return _run_screen(side_arr, target)
 
 
 def local(tokens, gate_weight, up_weight, down_weight):
@@ -12,7 +38,7 @@
         paired,
         preferred_element_type=jnp.float32,
     )
-    partial_sums = lax.all_to_all(every_token, "row", split_axis=1, concat_axis=2, tiled=True)
+    partial_sums = _begin_slots(every_token, "row", 1, 2)
     share_width = partial_sums.shape[2] // lax.axis_size("depth")
     summed = lax.psum(partial_sums, "depth")
     shares = lax.dynamic_slice_in_dim(summed, lax.axis_index("depth") * share_width, share_width, 2)

time: 811 us -> 786 us (0.969)
  blocking collectives: 119 us -> 0 us
  waiting for transfers between devices: 634 us -> 713 us
  starting transfers between devices: 0.12 us -> 16.5 us
    all_to_all x1 -> x0, blocking collectives: 119 us -> none  [local(): lax.all_to_all(every_token, 'row', split_axis=1, concat_axis=2, tiled=True)]
    ppermute x0 -> x7, waiting for transfers between devices: none -> 47.5 us  [_begin_slots(): lax.ppermute(spare, axis_id, [(pp, (pp + rr) % after) for pp in range(aft...]
    psum x1, waiting for transfers between devices: 27.2 us -> 58.4 us  [local(): summed = lax.psum(partial_sums, 'depth')]
    ppermute x0 -> x7, starting transfers between devices: none -> 16.4 us  [_begin_slots(): lax.ppermute(spare, axis_id, [(pp, (pp + rr) % after) for pp in range(aft...]
    all_to_all x1 -> x0, local copies, waits for them, and re-layouts: 8.69 us -> none  [local(): lax.all_to_all(every_token, 'row', split_axis=1, concat_axis=2, tiled=True)]
  transfers between devices with their start and end apart: 4 -> 11, of which waited for: 4 -> 7; matrix products, arithmetic and copies ran while one was open for 0% -> 1% of each run, Pallas kernels for 0% -> 0%
where the time goes in v1:
time: 786 us
  waiting for transfers between devices  713 us (91%)
  matrix products  24 us (3%)
  local copies, waits for them, and re-layouts  18 us (2%)
  starting transfers between devices  16.5 us (2%)
  between operations  13.3 us (2%)
    all_gather x1, waiting for transfers between devices, local(): lax.all_gather(down_weight, 'row', axis=1, tiled=True)  476 us
    all_gather x1, waiting for transfers between devices, local(): lax.all_gather(tokens, 'row', axis=0, tiled=True)  94 us
    psum x1, waiting for transfers between devices, local(): summed = lax.psum(partial_sums, 'depth')  58.4 us
    ppermute x7, waiting for transfers between devices, _begin_slots(): lax.ppermute(spare, axis_id, [(pp, (pp + rr) % after) for pp in range(aft...  47.5 us
    reduce_scatter x1, waiting for transfers between devices, local(): lax.psum_scatter(down_terms, ('col', 'depth'), scatter_dimension=1, tiled...  35.5 us
    ppermute x7, starting transfers between devices, _begin_slots(): lax.ppermute(spare, axis_id, [(pp, (pp + rr) % after) for pp in range(aft...  16.4 us
  transfers between devices with their start and end apart: 11, of which 7 were waited for; matrix products, arithmetic and copies ran while one was open for 1% of the time, Pallas kernels for 0%

profile of v1, /device:TPU:0, one launch (start us, length us, event | category | flops | bytes accessed | tf_op | source)
XLA Modules:
  0.0 786.1 jit_solution(4941203555601219812)
XLA Ops:
  7.4 94.0 %all-gather.3.cloned.1.call-done = bf16[1024,2688]{1,0:T(8,128)(2,1)} async-done(((bf16[128,2688]{1,0:T(8,128)(2,1)}), bf16[1024,2688]{1,0:T(8,128)(2,1)}) %all-gather.3.cloned.1.call-update) | async-done | bytes 5505040 | tf_op jit(solution)/shard_map/all_gather | solution.py:37
  101.4 10.6 %fusion = f32[2,576,1024]{2,1,0:T(8,128)S(1)} fusion(bf16[1,576,2688]{2,1,0:T(8,128)(2,1)} %bitcast.50, bf16[1,576,2688]{2,1,0:T(8,128)(2,1)} %bitcast.51, bf16[1024,2688]{1,0:T(8,128)(2,1)} %all-gather.3.cloned.1.call-done), kind=kOutput, calls=%fused_computation | convolution fusion | flops 6344884224 | bytes 16416768 | tf_op jit(solution)/shard_map/td,gfd->gtf/dot_general | solution.py:35
  112.0 1.2 copy.7
  113.2 1.1 copy-done
  114.3 3.6 constant_dynamic-slice_fusion
  119.0 2.4 collective-permute-start.2
  121.4 2.3 collective-permute-start.3
  124.3 5.0 bitcast_bitcast_fusion
  129.2 8.0 %collective-permute-done = f32[1,2,128,576]{2,3,0,1:T(8,128)} collective-permute-done((f32[1,2,128,576]{2,3,0,1:T(8,128)}, f32[1,2,128,576]{2,3,0,1:T(8,128)}, u32[]{:S(2)}, u32[]{:S(2)}) %collective-permute-start) | collective-permute-done | bytes 589856 | tf_op jit(solution)/shard_map/ppermute | solution.py:28
  137.2 2.0 constant_dynamic-update-slice_fusion.6
  139.2 10.0 %collective-permute-start.6 = (f32[1,2,128,576]{2,3,0,1:T(8,128)S(1)}, f32[1,2,128,576]{2,3,0,1:T(8,128)S(1)}, u32[]{:S(2)}, u32[]{:S(2)}) collective-permute-start(f32[1,2,128,576]{2,3,0,1:T(8,128)S(1)} %bitcast.44), channel_id=1, source_target_pairs={{0,28},{4,0},{8,4},{12,8},{16,12},{20,16},{24,20},{28,24},{1,29},{... | collective-permute-start | bytes 1769480 | tf_op jit(solution)/shard_map/ppermute | solution.py:28
  149.2 0.9 constant_dynamic-update-slice_fusion.5
  150.1 34.9 %collective-permute-done.2 = f32[1,2,128,576]{2,3,0,1:T(8,128)S(1)} collective-permute-done((f32[1,2,128,576]{2,3,0,1:T(8,128)S(1)}, f32[1,2,128,576]{2,3,0,1:T(8,128)S(1)}, u32[]{:S(2)}, u32[]{:S(2)}) %collective-permute-start.2) | collective-permute-done | bytes 589856 | tf_op jit(solution)/shard_map/ppermute | solution.py:28
  185.0 0.9 constant_dynamic-update-slice_fusion.4
  185.8 0.9 constant_dynamic-update-slice_fusion.3
  186.7 0.9 constant_dynamic-update-slice_fusion.2
  187.6 0.9 constant_dynamic-update-slice_fusion.1
  188.5 4.6 collective-permute-done.6
  193.1 0.9 constant_dynamic-update-slice_fusion
  194.7 58.4 %all-reduce.2.cloned.1.call-done = f32[2,128,4608]{1,2,0:T(8,128)} async-done(((f32[2,128,4608]{1,2,0:T(8,128)}), f32[2,128,4608]{1,2,0:T(8,128)}) %all-reduce.2.cloned.1.call-update) | async-done | bytes 4718608 | tf_op jit(solution)/shard_map/psum | solution.py:43
  253.1 475.7 %all-gather.5.cloned.1.call-done = bf16[2304,5376]{0,1:T(8,128)(2,1)} async-done(((bf16[2304,672]{0,1:T(8,128)(2,1)}), bf16[2304,5376]{0,1:T(8,128)(2,1)}) %all-gather.5.cloned.1.call-update) | async-done | bytes 24772624 | tf_op jit(solution)/shard_map/all_gather | solution.py:48
  728.9 13.3 %fusion.7 = f32[128,5376]{0,1:T(8,128)} fusion(bf16[2304,5376]{0,1:T(8,128)(2,1)} %all-gather.5.cloned.1.call-done, f32[2,128,4608]{1,2,0:T(8,128)} %all-reduce.2.cloned.1.call-done, s32[]{:T(128)S(6)} %add.162, s32[]{:T(128)S(6)} %select_n.133), kind=kOutput, calls=%fused_computation.10 | convolution fusion | flops 3172663296 | bytes 29884424 | tf_op jit(solution)/shard_map/dot_general | solution.py:46
  742.2 35.5 %reduce-scatter.2.cloned.1.call-done = f32[128,1344]{0,1:T(8,128)} async-done(((f32[128,5376]{0,1:T(8,128)}), f32[128,1344]{0,1:T(8,128)}) %reduce-scatter.2.cloned.1.call-update) | async-done | bytes 688144 | tf_op jit(solution)/shard_map/reduce_scatter | solution.py:51
  777.7 1.9 convert_element_type.7
  (17 shorter events, 3.2 us)
Async XLA Ops:
  6.5 94.9 %all-gather.3.cloned.1.call-start = ((), (), s32[]{:S(2)}) async-start(), calls=%async_computation.1 | async-start | bytes 6193152 | tf_op jit(solution)/shard_map/all_gather | solution.py:37
  7.3 245.9 %all-reduce.2.cloned.1.call-start = ((), (), s32[]{:S(2)}) async-start(), calls=%async_computation.2 | async-start | bytes 9437184 | tf_op jit(solution)/shard_map/psum | solution.py:43
  112.0 2.3 copy-start
  117.9 19.4 %collective-permute-start = (f32[1,2,128,576]{2,3,0,1:T(8,128)}, f32[1,2,128,576]{2,3,0,1:T(8,128)}, u32[]{:S(2)}, u32[]{:S(2)}) collective-permute-start(f32[1,2,128,576]{2,3,0,1:T(8,128)} %bitcast.5), channel_id=1, source_target_pairs={{0,4},{4,8},{8,12},{12,16},{16,20},{20,24},{24,28},{28,0},{1,5},{5... | collective-permute-start | bytes 1769480 | tf_op jit(solution)/shard_map/ppermute | solution.py:28
  118.4 20.8 %collective-permute-start.1 = (f32[1,2,128,576]{2,3,0,1:T(8,128)S(1)}, f32[1,2,128,576]{2,3,0,1:T(8,128)S(1)}, u32[]{:S(2)}, u32[]{:S(2)}) collective-permute-start(f32[1,2,128,576]{2,3,0,1:T(8,128)S(1)} %bitcast.49), channel_id=1, source_target_pairs={{0,8},{4,12},{8,16},{12,20},{16,24},{20,28},{24,0},{28,4},{1,9},{5... | collective-permute-start | bytes 1769480 | tf_op jit(solution)/shard_map/ppermute | solution.py:28
  119.0 66.0 %collective-permute-start.2 = (f32[1,2,128,576]{2,3,0,1:T(8,128)S(1)}, f32[1,2,128,576]{2,3,0,1:T(8,128)S(1)}, u32[]{:S(2)}, u32[]{:S(2)}) collective-permute-start(f32[1,2,128,576]{2,3,0,1:T(8,128)S(1)} %bitcast.48), channel_id=1, source_target_pairs={{0,12},{4,16},{8,20},{12,24},{16,28},{20,0},{24,4},{28,8},{1,13},{... | collective-permute-start | bytes 1769480 | tf_op jit(solution)/shard_map/ppermute | solution.py:28
  121.4 64.5 %collective-permute-start.3 = (f32[1,2,128,576]{2,3,0,1:T(8,128)S(1)}, f32[1,2,128,576]{2,3,0,1:T(8,128)S(1)}, u32[]{:S(2)}, u32[]{:S(2)}) collective-permute-start(f32[1,2,128,576]{2,3,0,1:T(8,128)S(1)} %bitcast.47), channel_id=1, source_target_pairs={{0,16},{4,20},{8,24},{12,28},{16,0},{20,4},{24,8},{28,12},{1,17},{... | collective-permute-start | bytes 1769480 | tf_op jit(solution)/shard_map/ppermute | solution.py:28
  123.7 63.0 %collective-permute-start.4 = (f32[1,2,128,576]{2,3,0,1:T(8,128)S(1)}, f32[1,2,128,576]{2,3,0,1:T(8,128)S(1)}, u32[]{:S(2)}, u32[]{:S(2)}) collective-permute-start(f32[1,2,128,576]{2,3,0,1:T(8,128)S(1)} %bitcast.46), channel_id=1, source_target_pairs={{0,20},{4,24},{8,28},{12,0},{16,4},{20,8},{24,12},{28,16},{1,21},{... | collective-permute-start | bytes 1769480 | tf_op jit(solution)/shard_map/ppermute | solution.py:28
  137.2 50.4 %collective-permute-start.5 = (f32[1,2,128,576]{2,3,0,1:T(8,128)S(1)}, f32[1,2,128,576]{2,3,0,1:T(8,128)S(1)}, u32[]{:S(2)}, u32[]{:S(2)}) collective-permute-start(f32[1,2,128,576]{2,3,0,1:T(8,128)S(1)} %bitcast.45), channel_id=1, source_target_pairs={{0,24},{4,28},{8,0},{12,4},{16,8},{20,12},{24,16},{28,20},{1,25},{... | collective-permute-start | bytes 1769480 | tf_op jit(solution)/shard_map/ppermute | solution.py:28
  139.2 53.9 %collective-permute-start.6 = (f32[1,2,128,576]{2,3,0,1:T(8,128)S(1)}, f32[1,2,128,576]{2,3,0,1:T(8,128)S(1)}, u32[]{:S(2)}, u32[]{:S(2)}) collective-permute-start(f32[1,2,128,576]{2,3,0,1:T(8,128)S(1)} %bitcast.44), channel_id=1, source_target_pairs={{0,28},{4,0},{8,4},{12,8},{16,12},{20,16},{24,20},{28,24},{1,29},{... | collective-permute-start | bytes 1769480 | tf_op jit(solution)/shard_map/ppermute | solution.py:28
  193.9 534.9 %all-gather.5.cloned.1.call-start = ((), (), s32[]{:S(2)}) async-start(), calls=%async_computation.3 | async-start | bytes 27869184 | tf_op jit(solution)/shard_map/all_gather | solution.py:48
  194.7 583.0 %reduce-scatter.2.cloned.1.call-start = ((), (), s32[]{:S(2)}) async-start(), calls=%async_computation.4 | async-start | bytes 3440640 | tf_op jit(solution)/shard_map/reduce_scatter | solution.py:51
Sparse Core Ops, SparseCore 0:
  9.5 91.8 all-gather.2
  194.1 59.0 all-reduce.1
  254.7 474.1 all-gather.4
  742.4 35.2 reduce-scatter.1
